TPU v7x, 256 devices: a 2x2x32 block of a 4x8x32 slice. The times are simulated.
256 devices in a mesh: groups: 4 (over y, x), dp: 2 (over core), seq: 32 (over z).
Axes of the slice: x: 2, y: 2, z: 32, core: 2. Of those that a mesh axis runs over, the one named last changes fastest.
The devices are a block of a 4x8x32 slice.
Arguments:
- history: bfloat16 [16, 3072, 1024], P(('groups', 'dp'), 'seq'), parts along dimension 0, may hold values from -20 to 20
- candidates: bfloat16 [8, 2048, 1024], P(('groups', 'dp'), 'seq'), parts along dimension 0, may hold values from -6 to 6
- lengths: int32 [16], P(('groups', 'dp')), parts along dimension 0, may hold values from 384 to 3072
- assignment: int32 [8, 2048], P(('groups', 'dp'), 'seq'), parts along dimension 0, may hold values from 0 to 1, as said below
- weight_in: bfloat16 [1024, 4096], replicated, may hold values from -0.1875 to 0.1875
- weight_out: bfloat16 [1024, 1024], replicated, may hold values from -0.1875 to 0.1875
- gain_in: float32 [1024], replicated, may hold values from 0.25 to 1.75
- gain_attn: float32 [1024], replicated, may hold values from 0.25 to 1.75
Outputs:
- history_out: bfloat16 [16, 3072, 1024], P(('groups', 'dp'), 'seq'), parts along dimension 0
- candidate_out: bfloat16 [8, 2048, 1024], P(('groups', 'dp'), 'seq'), parts along dimension 0
There are 4 independent parts, one for each index of `groups`. A program takes and returns all parts, laid end to end along the dimension named above; an argument that names none is the same for every part. Nothing has to cross between parts.
Inputs may be any that keep to these rules, and one draw needn't show every extreme that they name: `assignment`: of the 64 candidates of one device, at most 40 belong to either history; in every dp index some device has exactly 40 of the first and another exactly 40 of the second.
All inputs are finite; a program needn't handle non-finite values.
Results may differ from a plain program's by a relative error of at most 0.0075.
Values may be sent and summed in bfloat16 or wider, within the bound.
No kernel may reach another device: no remote copies, remote signals or barrier semaphores. Data moves between devices by JAX's collectives and lax.ppermute only.
A program may use at most 192 MiB of HBM per device.

v0:
```python
import functools

import jax
import jax.numpy as jnp
from jax import lax
from jax.experimental import pallas as pl
from jax.experimental.pallas import tpu as pltpu
from jax.sharding import PartitionSpec as P

H = 16
HD = 64
CAP = 40
LANES = 128
CAND_TOP = 24
CAND_LOW = CAP - CAND_TOP
HEADS_STEP = 4
GROUP = 8
F32 = jnp.float32
BF16 = jnp.bfloat16


def rms_apply(values, gain):
    return values * lax.rsqrt(jnp.mean(values * values, axis=-1, keepdims=True) + 1e-06) * gain


def silu(values):
    half = values * 0.5
    return half + half * jnp.tanh(half)


def swap_halves(values):
    return pltpu.roll(values, HD, 1)


def low_lanes(rows):
    return lax.broadcasted_iota(jnp.int32, (rows, LANES), 1) < HD


def join(first, second):
    return jnp.where(low_lanes(first.shape[0]), first, second)


def selection(owner_row, member):
    count = owner_row.shape[1]
    mine = (owner_row == member).astype(F32)
    before = (
        lax.broadcasted_iota(jnp.int32, (count, count), 0)
        < lax.broadcasted_iota(jnp.int32, (count, count), 1)
    ).astype(F32)
    rank = jnp.dot(jnp.broadcast_to(mine, (8, count)), before, preferred_element_type=F32)[0:1]
    rank = jnp.where(mine > 0.5, rank, -1.0)
    rows = lax.broadcasted_iota(jnp.int32, (2 * CAND_TOP, count), 0).astype(F32)
    return (rows == rank).astype(F32)


def project_kernel(
    axis,
    tok_share,
    lengths_ref,
    hist_ref,
    cand_ref,
    owner_ref,
    gain_ref,
    wg_ref,
    wq_ref,
    wk_ref,
    wv_ref,
    send_ref,
    gate_ref,
    cgate_ref,
    normed_ref,
):
    hist_rows = hist_ref.shape[0]
    hist_local = hist_rows // tok_share
    half = tok_share // 2
    first_token = lax.axis_index(axis) * tok_share

    @pl.when(pl.program_id(0) == 0)
    def _():
        gain = gain_ref[...]
        normed_ref[:hist_rows] = rms_apply(hist_ref[...].astype(F32), gain).astype(BF16)
        normed_ref[hist_rows:] = rms_apply(cand_ref[...].astype(F32), gain).astype(BF16)

    hist_normed = normed_ref[:hist_rows]
    keys = jnp.dot(hist_normed, wk_ref[...], preferred_element_type=F32)
    values = jnp.dot(hist_normed, wv_ref[...], preferred_element_type=F32)
    normed = normed_ref[...]
    query = jnp.dot(normed, wq_ref[...], preferred_element_type=F32)
    gate = silu(jnp.dot(normed, wg_ref[...], preferred_element_type=F32)).astype(BF16)
    gate_ref[...] = gate[:hist_rows]
    cgate_ref[...] = gate[hist_rows:]
    query = query.astype(BF16).astype(F32) * (0.5 * HD ** (-0.5))
    cand_query = query[hist_rows:].astype(BF16)
    for member in range(hist_local):
        rows = slice(member * tok_share, (member + 1) * tok_share)
        position = first_token + lax.broadcasted_iota(jnp.int32, (tok_share, LANES), 0)
        present = position < lengths_ref[member]
        picked = jnp.dot(
            selection(owner_ref[...], member).astype(BF16),
            cand_query,
            preferred_element_type=F32,
        )
        for pair in range(HEADS_STEP // 2):
            lanes = slice(pair * LANES, (pair + 1) * LANES)
            key_slab = jnp.where(present, keys[rows, lanes], 0.0)
            value_slab, query_slab = values[rows, lanes], query[rows, lanes]
            cand_slab = picked[:, lanes]
            even, odd = 2 * pair, 2 * pair + 1
            send_ref[member, even, :tok_share] = join(key_slab, swap_halves(value_slab)).astype(BF16)
            send_ref[member, odd, :tok_share] = join(swap_halves(key_slab), value_slab).astype(BF16)
            top, low = query_slab[:half], query_slab[half:]
            place = slice(tok_share, tok_share + half)
            send_ref[member, even, place] = join(top, swap_halves(low)).astype(BF16)
            send_ref[member, odd, place] = join(swap_halves(top), low).astype(BF16)
            top, low = cand_slab[:CAND_TOP], cand_slab[CAND_TOP:]
            place = slice(tok_share + half, tok_share + half + CAND_TOP)
            send_ref[member, even, place] = join(top, swap_halves(low)).astype(BF16)
            send_ref[member, odd, place] = join(swap_halves(top), low).astype(BF16)


def attend_kernel(tok_share, recv_ref, back_ref, vt_ref, q_ref, cq_ref, ot_ref, ct_ref):
    sources = recv_ref.shape[0]
    half = tok_share // 2
    groups = sources // GROUP
    keys_group, half_group = GROUP * tok_share, GROUP * half
    queries_group = 2 * half_group
    top_cands, low_cands = sources * CAND_TOP, sources * CAND_LOW
    cand_first = tok_share + half

    def keys_of(group):
        return recv_ref[group * GROUP : (group + 1) * GROUP, :tok_share].reshape(keys_group, LANES)

    def low_half(values):
        return jnp.where(low_lanes(values.shape[0]), values, 0.0).astype(BF16)

    for group in range(groups):
        members = slice(group * GROUP, (group + 1) * GROUP)
        vt_ref[group] = keys_of(group).T[HD:]
        packed = recv_ref[members, tok_share:cand_first].reshape(half_group, LANES).astype(F32)
        base = group * queries_group
        q_ref[base : base + half_group] = low_half(packed)
        q_ref[base + half_group : base + queries_group] = low_half(swap_halves(packed))
    packed = recv_ref[:, cand_first:].reshape(top_cands, LANES).astype(F32)
    cq_ref[:top_cands] = low_half(packed)
    packed = recv_ref[:, cand_first : cand_first + CAND_LOW].reshape(low_cands, LANES).astype(F32)
    cq_ref[top_cands:] = low_half(swap_halves(packed))

    def weigh(group, query, allowed=None):
        half_score = lax.dot_general(
            keys_of(group), query, (((1,), (1,)), ((), ())), preferred_element_type=F32
        )
        weight = half_score + half_score * jnp.tanh(half_score)
        if allowed is not None:
            weight = jnp.where(allowed, weight, 0.0)
        return jnp.dot(vt_ref[group], weight.astype(BF16), preferred_element_type=F32)

    for group in range(groups):
        part = weigh(group, cq_ref[...])
        ct_ref[...] = part if group == 0 else ct_ref[...] + part

    column = lax.broadcasted_iota(jnp.int32, (1, queries_group), 1)
    is_low = (column >= half_group).astype(jnp.int32)
    column = column - is_low * half_group
    source = jnp.zeros_like(column)
    for later in range(1, GROUP):
        source = source + (column >= later * half).astype(jnp.int32)
    position = source * half + column + is_low * half
    causal = lax.broadcasted_iota(jnp.int32, (keys_group, queries_group), 0) <= position
    for group in range(groups):
        base = group * queries_group
        own = slice(base, base + queries_group)
        part = weigh(group, q_ref[own], causal)
        ot_ref[:, own] = part if group == 0 else ot_ref[:, own] + part
        if group + 1 < groups:
            later = slice(base + queries_group, groups * queries_group)
            part = weigh(group, q_ref[later])
            ot_ref[:, later] = part if group == 0 else ot_ref[:, later] + part

    for group in range(groups):
        base = group * queries_group
        top = ot_ref[:, base : base + half_group]
        low = ot_ref[:, base + half_group : base + queries_group]
        joined = jnp.concatenate([top, low], axis=0).T.astype(BF16)
        back_ref[group * GROUP : (group + 1) * GROUP, :half] = joined.reshape(GROUP, half, LANES)
    top, low = ct_ref[:, :top_cands].T, ct_ref[:, top_cands:].T
    top = jnp.concatenate([top, jnp.zeros_like(top)], axis=1).reshape(sources, CAND_TOP, LANES)
    low = jnp.concatenate([jnp.zeros_like(low), low], axis=1).reshape(sources, CAND_LOW, LANES)
    back_ref[:, half : half + CAND_LOW] = (top[:, :CAND_LOW] + low).astype(BF16)
    back_ref[:, half + CAND_LOW :] = top[:, CAND_LOW:].astype(BF16)


def output_kernel(
    tok_share,
    back_ref,
    owner_ref,
    hist_ref,
    cand_ref,
    gate_ref,
    cgate_ref,
    gain_ref,
    weight_ref,
    hist_out_ref,
    cand_out_ref,
    rows_ref,
):
    half = tok_share // 2
    hist_rows = hist_ref.shape[0]
    hist_local = hist_rows // tok_share
    cand_rows = cand_ref.shape[0]
    cross = []
    for pair in range(H // 2):
        lanes = slice(pair * LANES, (pair + 1) * LANES)
        cross_slab = jnp.zeros((cand_rows, LANES), F32)
        for member in range(hist_local):
            base = member * tok_share
            even = back_ref[member * H + 2 * pair].astype(F32)
            odd = back_ref[member * H + 2 * pair + 1].astype(F32)
            upper = join(even, swap_halves(odd))
            lower = join(swap_halves(even), odd)
            rows_ref[base : base + half, lanes] = upper[:half]
            rows_ref[base + half : base + tok_share, lanes] = lower[:half]
            found = jnp.concatenate([upper[half:], lower[half:]], axis=0).astype(BF16)
            pick = selection(owner_ref[...], member).astype(BF16)
            cross_slab = cross_slab + lax.dot_general(
                pick, found, (((0,), (0,)), ((), ())), preferred_element_type=F32
            )
        rows_ref[hist_rows:, lanes] = cross_slab
    gain = gain_ref[...]
    attended = rows_ref[...]
    scaled = rms_apply(attended, gain)
    hist_gated = (scaled[:hist_rows] * gate_ref[...].astype(F32)).astype(BF16)
    cand_gated = (scaled[hist_rows:] * cgate_ref[...].astype(F32)).astype(BF16)
    gated = jnp.concatenate([hist_gated, cand_gated], axis=0)
    product = jnp.dot(gated, weight_ref[...], preferred_element_type=F32)
    hist_out_ref[...] = (hist_ref[...].astype(F32) + product[:hist_rows]).astype(BF16)
    cand_out_ref[...] = (cand_ref[...].astype(F32) + product[hist_rows:]).astype(BF16)


def per_device(history, candidates, lengths, assignment, weight_in, weight_out, gain_in, gain_attn):
    seq_devices = lax.axis_size("seq")
    hist_local, tok_share, width = history.shape
    cand_count = candidates.shape[1]
    half = tok_share // 2
    hist_rows = hist_local * tok_share
    items = hist_local * H
    assert items == seq_devices
    hist = history.reshape(hist_rows, width)
    cand = candidates.reshape(cand_count, width)
    gain_in = gain_in.reshape(1, width)
    gain_attn = gain_attn.reshape(1, width)
    send_rows = tok_share + half + CAND_TOP
    step_width = HEADS_STEP * HD
    steps = H // HEADS_STEP

    def whole(shape):
        return pl.BlockSpec(shape, lambda *_: (0,) * len(shape))

    def part(number):
        return pl.BlockSpec((width, step_width), lambda j: (0, number * steps + j))

    send, gate, cgate = pl.pallas_call(
        functools.partial(project_kernel, "seq", tok_share),
        grid=(steps,),
        in_specs=[
            pl.BlockSpec(memory_space=pltpu.SMEM),
            whole((hist_rows, width)),
            whole((cand_count, width)),
            whole((1, cand_count)),
            whole((1, width)),
            part(0),
            part(1),
            part(2),
            part(3),
        ],
        out_specs=[
            pl.BlockSpec((hist_local, HEADS_STEP, send_rows, LANES), lambda j: (0, j, 0, 0)),
            pl.BlockSpec((hist_rows, step_width), lambda j: (0, j)),
            pl.BlockSpec((cand_count, step_width), lambda j: (0, j)),
        ],
        out_shape=[
            jax.ShapeDtypeStruct((hist_local, H, send_rows, LANES), BF16),
            jax.ShapeDtypeStruct((hist_rows, width), BF16),
            jax.ShapeDtypeStruct((cand_count, width), BF16),
        ],
        scratch_shapes=[pltpu.VMEM((hist_rows + cand_count, width), BF16)],
        name="project",
    )(lengths, hist, cand, assignment, gain_in, weight_in, weight_in, weight_in, weight_in)
    recv = lax.all_to_all(
        send.reshape(items, send_rows, LANES), "seq", split_axis=0, concat_axis=0, tiled=True
    )
    length = seq_devices * tok_share
    back = pl.pallas_call(
        functools.partial(attend_kernel, tok_share),
        in_specs=[pl.BlockSpec(memory_space=pltpu.VMEM)],
        out_specs=pl.BlockSpec(memory_space=pltpu.VMEM),
        out_shape=jax.ShapeDtypeStruct((seq_devices, half + CAND_TOP, LANES), BF16),
        scratch_shapes=[
            pltpu.VMEM((seq_devices // GROUP, HD, GROUP * tok_share), BF16),
            pltpu.VMEM((length, LANES), BF16),
            pltpu.VMEM((seq_devices * CAP, LANES), BF16),
            pltpu.VMEM((HD, length), F32),
            pltpu.VMEM((HD, seq_devices * CAP), F32),
        ],
        name="attend",
    )(recv)
    home = lax.all_to_all(back, "seq", split_axis=0, concat_axis=0, tiled=True)
    hist_out, cand_out = pl.pallas_call(
        functools.partial(output_kernel, tok_share),
        out_shape=[
            jax.ShapeDtypeStruct((hist_rows, width), BF16),
            jax.ShapeDtypeStruct((cand_count, width), BF16),
        ],
        scratch_shapes=[pltpu.VMEM((hist_rows + cand_count, width), F32)],
        name="combine",
    )(home, assignment, hist, cand, gate, cgate, gain_attn, weight_out)
    return hist_out.reshape(history.shape), cand_out.reshape(candidates.shape)


def solution(mesh):
    in_specs = (
        P(("groups", "dp"), "seq", None),
        P(("groups", "dp"), "seq", None),
        P(("groups", "dp")),
        P(("groups", "dp"), "seq"),
        P(),
        P(),
        P(),
        P(),
    )
    out_specs = (P(("groups", "dp"), "seq", None), P(("groups", "dp"), "seq", None))
    return jax.shard_map(
        per_device, mesh=mesh, in_specs=in_specs, out_specs=out_specs, check_vma=False
    )
```

profile of v0, /device:TPU:37, one launch (start us, length us, event | category | flops | bytes accessed | tf_op | source)
XLA Modules:
  0.0 265.8 jit_solution(807186867294865429)
XLA Ops:
  0.6 7.9 %project.1 = (bf16[2,16,168,128]{3,2,1,0:T(8,128)(2,1)}, bf16[192,1024]{1,0:T(8,128)(2,1)}, bf16[64,1024]{1,0:T(8,128)(2,1)}) custom-call(s32[2]{0:T(128)} %lengths_ref.1, bf16[192,1024]{1,0:T(8,128)(2,1)} %bitcast.7, bf16[64,1024]{1,0:T(8,128)(2,1)} %bitcast.10, s32[1,64]{1,0:T(1,128)} %owner_ref.3, f32[1,1024]{1,0:T(1,128)} %bitcast.13, ...), custom_call_target="tpu_custom_call" | custom-call | tf_op jit(solution)/shard_map/project/pallas_call | solution.py:261
  8.5 169.6 %all_to_all.10.recv_ref = bf16[32,168,128]{2,1,0:T(8,128)(2,1)} all-to-all(bf16[32,168,128]{2,1,0:T(8,128)(2,1)} %bitcast.9), channel_id=1, replica_groups=mesh['groups'=4,'dp'=2,'seq'=32] {'seq'}, dimensions={0} | all-to-all | bytes 2752512 | tf_op jit(solution)/shard_map/all_to_all | solution.py:288
  178.1 12.1 %attend.1 = bf16[32,72,128]{2,1,0:T(8,128)(2,1)} custom-call(bf16[32,168,128]{2,1,0:T(8,128)(2,1)} %all_to_all.10.recv_ref), custom_call_target="tpu_custom_call" | custom-call | tf_op jit(solution)/shard_map/attend/pallas_call | solution.py:292
  190.2 71.2 %all_to_all.11.back_ref = bf16[32,72,128]{2,1,0:T(8,128)(2,1)} all-to-all(bf16[32,72,128]{2,1,0:T(8,128)(2,1)} %attend.1), channel_id=1, replica_groups=mesh['groups'=4,'dp'=2,'seq'=32] {'seq'}, dimensions={0} | all-to-all | bytes 1179648 | tf_op jit(solution)/shard_map/all_to_all | solution.py:306
  261.5 4.3 %combine.1 = (bf16[192,1024]{1,0:T(8,128)(2,1)}, bf16[64,1024]{1,0:T(8,128)(2,1)}) custom-call(bf16[32,72,128]{2,1,0:T(8,128)(2,1)} %all_to_all.11.back_ref, s32[1,64]{1,0:T(1,128)} %owner_ref.3, bf16[192,1024]{1,0:T(8,128)(2,1)} %bitcast.8, bf16[64,1024]{1,0:T(8,128)(2,1)} %bitcast.11, bf16[192,1024]{1,0:T(8,128)(2,1)} %get-tuple-element.8.gate_ref, ...), custom_call_target="tpu_custom_call" | custom-call | tf_op jit(solution)/shard_map/combine/pallas_call | solution.py:307
where the time goes:
time: 270 us; the launch traced here: 266 us
  blocking collectives  241 us (89%)
  Pallas kernels  24.3 us (9%)
    all_to_all x1, blocking collectives, per_device(): lax.all_to_all(send.reshape(items, send_rows, LANES), 'seq', split_axis=0...  170 us
    all_to_all x1, blocking collectives, per_device(): home = lax.all_to_all(back, 'seq', split_axis=0, concat_axis=0, tiled=True)  71.2 us
    pallas_call x1, Pallas kernels, per_device(): pl.pallas_call(functools.partial(attend_kernel, tok_share), in_specs=[pl....  12.1 us
    pallas_call x1, Pallas kernels, per_device(): pl.pallas_call(functools.partial(project_kernel, 'seq', tok_share), grid=...  7.91 us

commit v1 on v0

v1 whole, which is shorter than its diff:
```python
import functools

import jax
import jax.numpy as jnp
from jax import lax
from jax.experimental import pallas as pl
from jax.experimental.pallas import tpu as pltpu
from jax.sharding import PartitionSpec as P

H = 16
HD = 64
CAP = 40
LANES = 128
CAND_HALF = CAP // 2
CAND_PAD = 24
HEADS_STEP = 4
PARTS = 4
VMEM_LIMIT = 28 << 20
GROUP = 8
F32 = jnp.float32
BF16 = jnp.bfloat16


def rms_apply(values, gain):
    return values * lax.rsqrt(jnp.mean(values * values, axis=-1, keepdims=True) + 1e-06) * gain


def silu(values):
    half = values * 0.5
    return half + half * jnp.tanh(half)


def swap_halves(values):
    return pltpu.roll(values, HD, 1)


def low_lanes(rows):
    return lax.broadcasted_iota(jnp.int32, (rows, LANES), 1) < HD


def join(first, second):
    return jnp.where(low_lanes(first.shape[0]), first, second)


def selection(owner_row, member):
    count = owner_row.shape[1]
    mine = (owner_row == member).astype(F32)
    before = (
        lax.broadcasted_iota(jnp.int32, (count, count), 0)
        < lax.broadcasted_iota(jnp.int32, (count, count), 1)
    ).astype(F32)
    rank = jnp.dot(jnp.broadcast_to(mine, (8, count)), before, preferred_element_type=F32)[0:1]
    row = jnp.where(rank < CAND_HALF, rank, rank + (CAND_PAD - CAND_HALF))
    row = jnp.where(mine > 0.5, row, -1.0)
    rows = lax.broadcasted_iota(jnp.int32, (2 * CAND_PAD, count), 0).astype(F32)
    return (rows == row).astype(BF16)


def project_kernel(
    axis,
    tok_share,
    lengths_hbm,
    hist_hbm,
    cand_hbm,
    owner_hbm,
    gain_hbm,
    weight_hbm,
    send_ref,
    gate_ref,
    cgate_ref,
    lengths_ref,
    hist_ref,
    cand_ref,
    owner_ref,
    gain_ref,
    weight_ref,
    normed_ref,
    loaded,
    arrived,
):
    hist_rows, width = hist_ref.shape
    hist_local = hist_rows // tok_share
    half = tok_share // 2
    chunk = tok_share + half + CAND_HALF
    step_width = HEADS_STEP * HD
    steps = H // HEADS_STEP

    def fetch(step, part):
        start = part * width + step * step_width
        return pltpu.make_async_copy(
            weight_hbm.at[:, start : start + step_width],
            weight_ref.at[step, part],
            arrived.at[step, part],
        )

    loads = [
        pltpu.make_async_copy(source, target, loaded.at[number])
        for number, (source, target) in enumerate(
            (
                (gain_hbm, gain_ref),
                (hist_hbm, hist_ref),
                (cand_hbm, cand_ref),
                (owner_hbm, owner_ref),
                (lengths_hbm, lengths_ref),
            )
        )
    ]
    for load in loads:
        load.start()
    for step in range(steps):
        for part in (2, 3, 1, 0):
            fetch(step, part).start()
    for load in loads:
        load.wait()
    gain = gain_ref[...]
    normed_ref[:hist_rows] = rms_apply(hist_ref[...].astype(F32), gain).astype(BF16)
    normed_ref[hist_rows:] = rms_apply(cand_ref[...].astype(F32), gain).astype(BF16)
    picks = [selection(owner_ref[...], member) for member in range(hist_local)]
    position = lax.axis_index(axis) * tok_share + lax.broadcasted_iota(jnp.int32, (tok_share, LANES), 0)

    for step in range(steps):

        def times(rows, part):
            fetch(step, part).wait()
            return jnp.dot(normed_ref[:rows], weight_ref[step, part], preferred_element_type=F32)

        all_rows = normed_ref.shape[0]
        keys = times(hist_rows, 2)
        values = times(hist_rows, 3)
        query = times(all_rows, 1).astype(BF16).astype(F32) * (0.5 * HD ** (-0.5))
        cand_query = query[hist_rows:].astype(BF16)
        for member in range(hist_local):
            rows = slice(member * tok_share, (member + 1) * tok_share)
            picked = jnp.dot(picks[member], cand_query, preferred_element_type=F32)
            present = position < lengths_ref[member]
            for pair in range(HEADS_STEP // 2):
                lanes = slice(pair * LANES, (pair + 1) * LANES)
                key_slab = jnp.where(present, keys[rows, lanes], 0.0)
                value_slab, query_slab, cand_slab = values[rows, lanes], query[rows, lanes], picked[:, lanes]
                even = (member * H + step * HEADS_STEP + 2 * pair) * chunk
                odd = even + chunk
                send_ref[even : even + tok_share] = join(key_slab, swap_halves(value_slab)).astype(BF16)
                send_ref[odd : odd + tok_share] = join(swap_halves(key_slab), value_slab).astype(BF16)
                top, low = query_slab[:half], query_slab[half:]
                even, odd = even + tok_share, odd + tok_share
                send_ref[even : even + half] = join(top, swap_halves(low)).astype(BF16)
                send_ref[odd : odd + half] = join(swap_halves(top), low).astype(BF16)
                top, low = cand_slab[:CAND_PAD], cand_slab[CAND_PAD:]
                even, odd = even + half, odd + half
                send_ref[even : even + CAND_HALF] = join(top, swap_halves(low)).astype(BF16)[:CAND_HALF]
                send_ref[odd : odd + CAND_HALF] = join(swap_halves(top), low).astype(BF16)[:CAND_HALF]
        gate = silu(times(all_rows, 0)).astype(BF16)
        columns = slice(step * step_width, (step + 1) * step_width)
        gate_ref[:, columns] = gate[:hist_rows]
        cgate_ref[:, columns] = gate[hist_rows:]


def attend_kernel(tok_share, recv_ref, back_ref, kv_ref, vt_ref, q_ref, cq_ref, ot_ref, ct_ref):
    half = tok_share // 2
    chunk, back_chunk = tok_share + half + CAND_HALF, half + CAND_HALF
    sources = recv_ref.shape[0] // chunk
    groups = sources // GROUP
    keys_group, half_group = GROUP * tok_share, GROUP * half
    queries_group = 2 * half_group
    cands = sources * CAND_HALF

    def keys_of(group):
        return kv_ref[group * keys_group : (group + 1) * keys_group]

    def low_half(values):
        return jnp.where(low_lanes(values.shape[0]), values, 0.0).astype(BF16)

    for source in range(sources):
        base = source * chunk
        kv_ref[source * tok_share : (source + 1) * tok_share] = recv_ref[base : base + tok_share]
        base = base + tok_share
        packed = recv_ref[base : base + half].astype(F32)
        place = source // GROUP * queries_group + source % GROUP * half
        q_ref[place : place + half] = low_half(packed)
        q_ref[place + half_group : place + half_group + half] = low_half(swap_halves(packed))
        base = base + half
        packed = recv_ref[base : base + CAND_HALF].astype(F32)
        place = source * CAND_HALF
        cq_ref[place : place + CAND_HALF] = low_half(packed)
        cq_ref[cands + place : cands + place + CAND_HALF] = low_half(swap_halves(packed))
    for group in range(groups):
        vt_ref[group] = keys_of(group).T[HD:]

    def weigh(group, query, allowed=None):
        half_score = lax.dot_general(
            keys_of(group), query, (((1,), (1,)), ((), ())), preferred_element_type=F32
        )
        weight = half_score + half_score * jnp.tanh(half_score)
        if allowed is not None:
            weight = jnp.where(allowed, weight, 0.0)
        return jnp.dot(vt_ref[group], weight.astype(BF16), preferred_element_type=F32)

    for group in range(groups):
        part = weigh(group, cq_ref[...])
        ct_ref[...] = part if group == 0 else ct_ref[...] + part

    column = lax.broadcasted_iota(jnp.int32, (1, queries_group), 1)
    is_low = (column >= half_group).astype(jnp.int32)
    column = column - is_low * half_group
    source = jnp.zeros_like(column)
    for later in range(1, GROUP):
        source = source + (column >= later * half).astype(jnp.int32)
    position = source * half + column + is_low * half
    causal = lax.broadcasted_iota(jnp.int32, (keys_group, queries_group), 0) <= position
    for group in range(groups):
        base = group * queries_group
        own = slice(base, base + queries_group)
        part = weigh(group, q_ref[own], causal)
        ot_ref[:, own] = part if group == 0 else ot_ref[:, own] + part
        if group + 1 < groups:
            later = slice(base + queries_group, groups * queries_group)
            part = weigh(group, q_ref[later])
            ot_ref[:, later] = part if group == 0 else ot_ref[:, later] + part

    for group in range(groups):
        base = group * queries_group
        top = ot_ref[:, base : base + half_group]
        low = ot_ref[:, base + half_group : base + queries_group]
        joined = jnp.concatenate([top, low], axis=0).T.astype(BF16)
        for member in range(GROUP):
            place = (group * GROUP + member) * back_chunk
            back_ref[place : place + half] = joined[member * half : (member + 1) * half]
    joined = jnp.concatenate([ct_ref[:, :cands], ct_ref[:, cands:]], axis=0).T.astype(BF16)
    for source in range(sources):
        place = source * back_chunk + half
        back_ref[place : place + CAND_HALF] = joined[source * CAND_HALF : (source + 1) * CAND_HALF]


def output_kernel(
    tok_share,
    back_ref,
    owner_ref,
    hist_ref,
    cand_ref,
    gate_ref,
    cgate_ref,
    gain_ref,
    weight_ref,
    hist_out_ref,
    cand_out_ref,
    rows_ref,
):
    half = tok_share // 2
    hist_rows = hist_ref.shape[0]
    hist_local = hist_rows // tok_share
    cand_rows = cand_ref.shape[0]
    chunk = half + CAND_HALF
    picks = [selection(owner_ref[...], member) for member in range(hist_local)]
    fill = jnp.zeros((CAND_PAD - CAND_HALF, LANES), F32)
    for pair in range(H // 2):
        lanes = slice(pair * LANES, (pair + 1) * LANES)
        cross_slab = jnp.zeros((cand_rows, LANES), F32)
        for member in range(hist_local):
            base = member * tok_share
            first = (member * H + 2 * pair) * chunk
            even = back_ref[first : first + half].astype(F32)
            odd = back_ref[first + chunk : first + chunk + half].astype(F32)
            rows_ref[base : base + half, lanes] = join(even, swap_halves(odd))
            rows_ref[base + half : base + tok_share, lanes] = join(swap_halves(even), odd)
            first = first + half
            even = back_ref[first : first + CAND_HALF].astype(F32)
            odd = back_ref[first + chunk : first + chunk + CAND_HALF].astype(F32)
            upper, lower = join(even, swap_halves(odd)), join(swap_halves(even), odd)
            found = jnp.concatenate([upper, fill, lower, fill], axis=0).astype(BF16)
            cross_slab = cross_slab + lax.dot_general(
                picks[member], found, (((0,), (0,)), ((), ())), preferred_element_type=F32
            )
        rows_ref[hist_rows:, lanes] = cross_slab
    gain = gain_ref[...]
    attended = rows_ref[...]
    scaled = rms_apply(attended, gain)
    hist_gated = (scaled[:hist_rows] * gate_ref[...].astype(F32)).astype(BF16)
    cand_gated = (scaled[hist_rows:] * cgate_ref[...].astype(F32)).astype(BF16)
    gated = jnp.concatenate([hist_gated, cand_gated], axis=0)
    product = jnp.dot(gated, weight_ref[...], preferred_element_type=F32)
    hist_out_ref[...] = (hist_ref[...].astype(F32) + product[:hist_rows]).astype(BF16)
    cand_out_ref[...] = (cand_ref[...].astype(F32) + product[hist_rows:]).astype(BF16)


def per_device(history, candidates, lengths, assignment, weight_in, weight_out, gain_in, gain_attn):
    seq_devices = lax.axis_size("seq")
    hist_local, tok_share, width = history.shape
    cand_count = candidates.shape[1]
    half = tok_share // 2
    hist_rows = hist_local * tok_share
    items = hist_local * H
    assert items == seq_devices
    hist = history.reshape(hist_rows, width)
    cand = candidates.reshape(cand_count, width)
    gain_in = gain_in.reshape(1, width)
    gain_attn = gain_attn.reshape(1, width)
    send_rows, back_rows = tok_share + half + CAND_HALF, half + CAND_HALF
    length = seq_devices * tok_share
    params = pltpu.CompilerParams(vmem_limit_bytes=VMEM_LIMIT)
    vmem = pl.BlockSpec(memory_space=pltpu.VMEM)

    def exchange(rows):
        pairs = rows.reshape(items, rows.shape[0] // items // 2, 2, LANES)
        moved = lax.all_to_all(pairs, "seq", split_axis=0, concat_axis=0, tiled=True)
        return pltpu.with_memory_space_constraint(moved.reshape(rows.shape), pltpu.VMEM)

    send, gate, cgate = pl.pallas_call(
        functools.partial(project_kernel, "seq", tok_share),
        in_specs=[pl.BlockSpec(memory_space=pltpu.HBM)] * 6,
        out_specs=[vmem] * 3,
        out_shape=[
            pltpu.VMEM((items * send_rows, LANES), BF16),
            jax.ShapeDtypeStruct((hist_rows, width), BF16),
            jax.ShapeDtypeStruct((cand_count, width), BF16),
        ],
        scratch_shapes=[
            pltpu.SMEM(lengths.shape, lengths.dtype),
            pltpu.VMEM(hist.shape, BF16),
            pltpu.VMEM(cand.shape, BF16),
            pltpu.VMEM(assignment.shape, assignment.dtype),
            pltpu.VMEM(gain_in.shape, F32),
            pltpu.VMEM((H // HEADS_STEP, PARTS, width, HEADS_STEP * HD), BF16),
            pltpu.VMEM((hist_rows + cand_count, width), BF16),
            pltpu.SemaphoreType.DMA((5,)),
            pltpu.SemaphoreType.DMA((H // HEADS_STEP, PARTS)),
        ],
        compiler_params=params,
        name="project",
    )(lengths, hist, cand, assignment, gain_in, weight_in)
    back = pl.pallas_call(
        functools.partial(attend_kernel, tok_share),
        in_specs=[vmem],
        out_specs=vmem,
        out_shape=pltpu.VMEM((items * back_rows, LANES), BF16),
        scratch_shapes=[
            pltpu.VMEM((length, LANES), BF16),
            pltpu.VMEM((seq_devices // GROUP, HD, GROUP * tok_share), BF16),
            pltpu.VMEM((length, LANES), BF16),
            pltpu.VMEM((seq_devices * CAP, LANES), BF16),
            pltpu.VMEM((HD, length), F32),
            pltpu.VMEM((HD, seq_devices * CAP), F32),
        ],
        compiler_params=params,
        name="attend",
    )(exchange(send))
    hist_out, cand_out = pl.pallas_call(
        functools.partial(output_kernel, tok_share),
        in_specs=[vmem] * 8,
        out_specs=[vmem] * 2,
        out_shape=[
            jax.ShapeDtypeStruct((hist_rows, width), BF16),
            jax.ShapeDtypeStruct((cand_count, width), BF16),
        ],
        scratch_shapes=[pltpu.VMEM((hist_rows + cand_count, width), F32)],
        compiler_params=params,
        name="combine",
    )(exchange(back), assignment, hist, cand, gate, cgate, gain_attn, weight_out)
    return hist_out.reshape(history.shape), cand_out.reshape(candidates.shape)


def solution(mesh):
    in_specs = (
        P(("groups", "dp"), "seq", None),
        P(("groups", "dp"), "seq", None),
        P(("groups", "dp")),
        P(("groups", "dp"), "seq"),
        P(),
        P(),
        P(),
        P(),
    )
    out_specs = (P(("groups", "dp"), "seq", None), P(("groups", "dp"), "seq", None))
    return jax.shard_map(
        per_device, mesh=mesh, in_specs=in_specs, out_specs=out_specs, check_vma=False
    )
```

time: 270 us -> 267 us (0.989)
  local copies, waits for them, and re-layouts: 0 us -> 7.29 us
  blocking collectives: 241 us -> 234 us
  Pallas kernels: 24.3 us -> 21.1 us
    unnamed x0 -> x22, local copies, waits for them, and re-layouts: none -> 7.29 us
    all_to_all x2, blocking collectives: 241 us -> 234 us  [exchange(): lax.all_to_all(pairs, 'seq', split_axis=0, concat_axis=0, tiled=True)]
    pallas_call x3, Pallas kernels: 24.3 us -> 21.1 us  [the longest x1 10.1 us: per_device(): pl.pallas_call(functools.partial(attend_kernel, tok_share), in_specs=[vme...]
where the time goes in v1:
time: 267 us; the launch traced here: 263 us
  blocking collectives  234 us (88%)
  Pallas kernels  21.1 us (8%)
  local copies, waits for them, and re-layouts  7.29 us (3%)
    all_to_all x2, blocking collectives, exchange(): lax.all_to_all(pairs, 'seq', split_axis=0, concat_axis=0, tiled=True)  234 us
    pallas_call x1, Pallas kernels, per_device(): pl.pallas_call(functools.partial(attend_kernel, tok_share), in_specs=[vme...  10.1 us
    pallas_call x1, Pallas kernels, per_device(): pl.pallas_call(functools.partial(project_kernel, 'seq', tok_share), in_sp...  9.02 us
    unnamed x22, local copies, waits for them, and re-layouts  7.29 us

profile of v1, /device:TPU:37, one launch (start us, length us, event | category | flops | bytes accessed | tf_op | source)
XLA Modules:
  0.0 263.5 jit_solution(4100048471161303874)
XLA Ops:
  0.6 0.0 copy-start
  0.6 3.4 %copy-done = bf16[1024,4096]{1,0:T(8,128)(2,1)S(1)} copy-done((bf16[1024,4096]{1,0:T(8,128)(2,1)S(1)}, bf16[1024,4096]{1,0:T(8,128)(2,1)}, u32[]{:S(2)}) %copy-start) | copy-done | bytes 8388632
  4.0 0.0 copy-start.2
  4.0 1.0 copy-done.2
  5.0 0.0 copy-start.4
  5.0 0.9 copy-done.4
  5.9 0.0 copy-start.6
  5.9 0.7 copy-done.6
  6.6 0.0 copy-start.8
  6.6 0.7 copy-done.8
  7.3 0.0 copy-start.10
  7.3 0.7 copy-done.10
  7.9 9.0 %project.1 = (bf16[5248,128]{1,0:T(8,128)(2,1)S(1)}, bf16[192,1024]{1,0:T(8,128)(2,1)S(1)}, bf16[64,1024]{1,0:T(8,128)(2,1)S(1)}) custom-call(s32[2]{0:T(128)S(1)} %copy-done.10, bf16[192,1024]{1,0:T(8,128)(2,1)S(1)} %bitcast.13, bf16[64,1024]{1,0:T(8,128)(2,1)S(1)} %bitcast.16, s32[1,64]{1,0:T(1,128)S(1)} %copy-done.8, f32[1,1024]{1,0:T(1,128)S(1)} %bitcast.18, ...), custom_call_target="tpu_custom_call" | custom-call | tf_op jit(solution)/shard_map/project/pallas_call | solution.py:307
  16.9 166.4 %all_to_all.10 = bf16[32,82,2,128]{3,2,1,0:T(2,128)(2,1)S(1)} all-to-all(bf16[32,82,2,128]{3,2,1,0:T(2,128)(2,1)S(1)} %bitcast.15), channel_id=1, replica_groups=mesh['groups'=4,'dp'=2,'seq'=32] {'seq'}, dimensions={0} | all-to-all | bytes 2686976 | tf_op jit(solution)/shard_map/all_to_all | solution.py:304
  183.3 0.0 copy-start.1
  183.3 0.0 copy-start.9
  183.3 10.1 %attend.1 = bf16[2176,128]{1,0:T(8,128)(2,1)S(1)} custom-call(bf16[5248,128]{1,0:T(8,128)(2,1)S(1)} %bitcast.10), custom_call_target="tpu_custom_call" | custom-call | tf_op jit(solution)/shard_map/attend/pallas_call | solution.py:330
  193.4 68.1 %all_to_all.11 = bf16[32,34,2,128]{3,2,1,0:T(2,128)(2,1)S(1)} all-to-all(bf16[32,34,2,128]{3,2,1,0:T(2,128)(2,1)S(1)} %bitcast.12), channel_id=1, replica_groups=mesh['groups'=4,'dp'=2,'seq'=32] {'seq'}, dimensions={0} | all-to-all | bytes 1114112 | tf_op jit(solution)/shard_map/all_to_all | solution.py:304
  261.5 0.0 copy-done.1
  261.5 0.0 copy-done.3
  261.5 0.0 copy-done.5
  261.5 0.0 copy-done.7
  261.5 0.0 copy-done.9
  261.5 2.0 combine.1
  (3 shorter events, 0.0 us)
Async XLA Ops:
  0.6 3.4 %copy-start = (bf16[1024,4096]{1,0:T(8,128)(2,1)S(1)}, bf16[1024,4096]{1,0:T(8,128)(2,1)}, u32[]{:S(2)}) copy-start(bf16[1024,4096]{1,0:T(8,128)(2,1)} %weight_hbm.1) | copy-start | bytes 25165828
  4.0 1.0 copy-start.2
  5.0 0.9 copy-start.4
  5.9 0.7 copy-start.6
  6.6 0.7 copy-start.8
  7.3 0.7 copy-start.10
  183.3 78.2 %copy-start.1 = (bf16[1024,1024]{1,0:T(8,128)(2,1)S(1)}, bf16[1024,1024]{1,0:T(8,128)(2,1)}, u32[]{:S(2)}) copy-start(bf16[1024,1024]{1,0:T(8,128)(2,1)} %weight_ref.1) | copy-start | bytes 6291460
  183.3 78.2 %copy-start.3 = (bf16[2,96,1024]{2,1,0:T(8,128)(2,1)S(1)}, bf16[2,96,1024]{2,1,0:T(8,128)(2,1)}, u32[]{:S(2)}) copy-start(bf16[2,96,1024]{2,1,0:T(8,128)(2,1)} %param.8) | copy-start | bytes 1179652
  183.3 78.2 %copy-start.5 = (bf16[1,64,1024]{2,1,0:T(8,128)(2,1)S(1)}, bf16[1,64,1024]{2,1,0:T(8,128)(2,1)}, u32[]{:S(2)}) copy-start(bf16[1,64,1024]{2,1,0:T(8,128)(2,1)} %param.9) | copy-start | bytes 393220
  183.3 78.2 %copy-start.7 = (f32[1024]{0:T(1024)S(1)}, f32[1024]{0:T(1024)}, u32[]{:S(2)}) copy-start(f32[1024]{0:T(1024)} %param.15) | copy-start | bytes 12292
  183.3 78.2 %copy-start.9 = (s32[1,64]{1,0:T(1,128)S(1)}, s32[1,64]{1,0:T(1,128)}, u32[]{:S(2)}) copy-start(s32[1,64]{1,0:T(1,128)} %owner_ref.1) | copy-start | bytes 772

commit v2 on v1

--- a/solution.py
+++ b/solution.py
@@ -13,7 +13,7 @@
 LANES = 128
 CAND_HALF = CAP // 2
 CAND_PAD = 24
-HEADS_STEP = 4
+HEADS_STEP = 16
 PARTS = 4
 VMEM_LIMIT = 28 << 20
 GROUP = 8
@@ -326,7 +326,12 @@
         ],
         compiler_params=params,
         name="project",
-    )(lengths, hist, cand, assignment, gain_in, weight_in)
+    )(
+        *(
+            pltpu.with_memory_space_constraint(argument, pltpu.HBM)
+            for argument in (lengths, hist, cand, assignment, gain_in, weight_in)
+        )
+    )
     back = pl.pallas_call(
         functools.partial(attend_kernel, tok_share),
         in_specs=[vmem],

time: 267 us -> 256 us (0.959)
  local copies, waits for them, and re-layouts: 7.29 us -> 0.02 us
  Pallas kernels: 21.1 us -> 17.5 us
    unnamed x22 -> x10, local copies, waits for them, and re-layouts: 7.29 us -> 0.02 us
    pallas_call x1, Pallas kernels: 9.02 us -> 5.51 us  [per_device(): pl.pallas_call(functools.partial(project_kernel, 'seq', tok_share), in_sp...]
where the time goes in v2:
time: 256 us; the launch traced here: 253 us
  blocking collectives  234 us (91%)
  Pallas kernels  17.5 us (7%)
    all_to_all x2, blocking collectives, exchange(): lax.all_to_all(pairs, 'seq', split_axis=0, concat_axis=0, tiled=True)  234 us
    pallas_call x1, Pallas kernels, per_device(): pl.pallas_call(functools.partial(attend_kernel, tok_share), in_specs=[vme...  10.1 us
    pallas_call x1, Pallas kernels, per_device(): pl.pallas_call(functools.partial(project_kernel, 'seq', tok_share), in_sp...  5.51 us

profile of v2, /device:TPU:37, one launch (start us, length us, event | category | flops | bytes accessed | tf_op | source)
XLA Modules:
  0.0 252.7 jit_solution(12312744612958790478)
XLA Ops:
  0.6 5.5 %project.1 = (bf16[5248,128]{1,0:T(8,128)(2,1)S(1)}, bf16[192,1024]{1,0:T(8,128)(2,1)S(1)}, bf16[64,1024]{1,0:T(8,128)(2,1)S(1)}) custom-call(s32[2]{0:T(128)} %lengths_hbm.1, bf16[192,1024]{1,0:T(8,128)(2,1)} %bitcast.13, bf16[64,1024]{1,0:T(8,128)(2,1)} %bitcast.16, s32[1,64]{1,0:T(1,128)} %owner_ref.1, f32[1,1024]{1,0:T(1,128)} %bitcast.19, ...), custom_call_target="tpu_custom_call" | custom-call | tf_op jit(solution)/shard_map/project/pallas_call | solution.py:307
  6.1 166.4 %all_to_all.10 = bf16[32,82,2,128]{3,2,1,0:T(2,128)(2,1)S(1)} all-to-all(bf16[32,82,2,128]{3,2,1,0:T(2,128)(2,1)S(1)} %bitcast.15), channel_id=1, replica_groups=mesh['groups'=4,'dp'=2,'seq'=32] {'seq'}, dimensions={0} | all-to-all | bytes 2686976 | tf_op jit(solution)/shard_map/all_to_all | solution.py:304
  172.5 0.0 copy-start
  172.5 0.0 copy-start.1
  172.5 0.0 copy-start.2
  172.5 0.0 copy-start.3
  172.5 0.0 copy-start.4
  172.5 10.1 %attend.1 = bf16[2176,128]{1,0:T(8,128)(2,1)S(1)} custom-call(bf16[5248,128]{1,0:T(8,128)(2,1)S(1)} %bitcast.10), custom_call_target="tpu_custom_call" | custom-call | tf_op jit(solution)/shard_map/attend/pallas_call | solution.py:335
  182.6 68.1 %all_to_all.11 = bf16[32,34,2,128]{3,2,1,0:T(2,128)(2,1)S(1)} all-to-all(bf16[32,34,2,128]{3,2,1,0:T(2,128)(2,1)S(1)} %bitcast.12), channel_id=1, replica_groups=mesh['groups'=4,'dp'=2,'seq'=32] {'seq'}, dimensions={0} | all-to-all | bytes 1114112 | tf_op jit(solution)/shard_map/all_to_all | solution.py:304
  250.7 0.0 copy-done
  250.7 0.0 copy-done.1
  250.7 0.0 copy-done.2
  250.7 0.0 copy-done.3
  250.7 0.0 copy-done.4
  250.7 2.0 combine.1
Async XLA Ops:
  172.5 78.2 %copy-start = (bf16[1024,1024]{1,0:T(8,128)(2,1)S(1)}, bf16[1024,1024]{1,0:T(8,128)(2,1)}, u32[]{:S(2)}) copy-start(bf16[1024,1024]{1,0:T(8,128)(2,1)} %weight_ref.1) | copy-start | bytes 6291460
  172.5 78.2 %copy-start.1 = (bf16[2,96,1024]{2,1,0:T(8,128)(2,1)S(1)}, bf16[2,96,1024]{2,1,0:T(8,128)(2,1)}, u32[]{:S(2)}) copy-start(bf16[2,96,1024]{2,1,0:T(8,128)(2,1)} %param.8) | copy-start | bytes 1179652
  172.5 78.2 %copy-start.2 = (bf16[1,64,1024]{2,1,0:T(8,128)(2,1)S(1)}, bf16[1,64,1024]{2,1,0:T(8,128)(2,1)}, u32[]{:S(2)}) copy-start(bf16[1,64,1024]{2,1,0:T(8,128)(2,1)} %param.9) | copy-start | bytes 393220
  172.5 78.2 %copy-start.3 = (f32[1024]{0:T(1024)S(1)}, f32[1024]{0:T(1024)}, u32[]{:S(2)}) copy-start(f32[1024]{0:T(1024)} %param.15) | copy-start | bytes 12292
  172.5 78.2 %copy-start.4 = (s32[1,64]{1,0:T(1,128)S(1)}, s32[1,64]{1,0:T(1,128)}, u32[]{:S(2)}) copy-start(s32[1,64]{1,0:T(1,128)} %owner_ref.1) | copy-start | bytes 772

commit v3 on v2

--- a/solution.py
+++ b/solution.py
@@ -16,6 +16,7 @@
 HEADS_STEP = 16
 PARTS = 4
 VMEM_LIMIT = 28 << 20
+STAGGER_NS = 35_000
 GROUP = 8
 F32 = jnp.float32
 BF16 = jnp.bfloat16
@@ -58,6 +59,7 @@
 
 def project_kernel(
     axis,
+    stagger_axis,
     tok_share,
     lengths_hbm,
     hist_hbm,
@@ -112,6 +114,10 @@
             fetch(step, part).start()
     for load in loads:
         load.wait()
+    @pl.when(lax.axis_index(stagger_axis) > 0)
+    def _():
+        pl.delay(STAGGER_NS)
+
     gain = gain_ref[...]
     normed_ref[:hist_rows] = rms_apply(hist_ref[...].astype(F32), gain).astype(BF16)
     normed_ref[hist_rows:] = rms_apply(cand_ref[...].astype(F32), gain).astype(BF16)
@@ -305,7 +311,7 @@
         return pltpu.with_memory_space_constraint(moved.reshape(rows.shape), pltpu.VMEM)
 
     send, gate, cgate = pl.pallas_call(
-        functools.partial(project_kernel, "seq", tok_share),
+        functools.partial(project_kernel, "seq", "dp", tok_share),
         in_specs=[pl.BlockSpec(memory_space=pltpu.HBM)] * 6,
         out_specs=[vmem] * 3,
         out_shape=[

time: 256 us -> 236 us (0.922); the launches traced: 253 us -> 235 us
  blocking collectives: 234 us -> 182 us
  Pallas kernels: 17.5 us -> 52.5 us
    all_to_all x2, blocking collectives: 234 us -> 182 us  [exchange(): lax.all_to_all(pairs, 'seq', split_axis=0, concat_axis=0, tiled=True)]
    pallas_call x1, Pallas kernels: 5.51 us -> 40.5 us  [per_device(): pl.pallas_call(functools.partial(project_kernel, 'seq', 'dp', tok_share),...]
where the time goes in v3:
time: 236 us; the launch traced here: 235 us
  blocking collectives  182 us (77%)
  Pallas kernels  52.5 us (22%)
    all_to_all x2, blocking collectives, exchange(): lax.all_to_all(pairs, 'seq', split_axis=0, concat_axis=0, tiled=True)  182 us
    pallas_call x1, Pallas kernels, per_device(): pl.pallas_call(functools.partial(project_kernel, 'seq', 'dp', tok_share),...  40.5 us
    pallas_call x1, Pallas kernels, per_device(): pl.pallas_call(functools.partial(attend_kernel, tok_share), in_specs=[vme...  10.1 us

profile of v3, /device:TPU:37, one launch (start us, length us, event | category | flops | bytes accessed | tf_op | source)
XLA Modules:
  0.0 235.4 jit_solution(9718842266822506554)
XLA Ops:
  0.6 40.5 %project.1 = (bf16[5248,128]{1,0:T(8,128)(2,1)S(1)}, bf16[192,1024]{1,0:T(8,128)(2,1)S(1)}, bf16[64,1024]{1,0:T(8,128)(2,1)S(1)}) custom-call(s32[2]{0:T(128)} %lengths_hbm.1, bf16[192,1024]{1,0:T(8,128)(2,1)} %bitcast.13, bf16[64,1024]{1,0:T(8,128)(2,1)} %bitcast.16, s32[1,64]{1,0:T(1,128)} %owner_ref.1, f32[1,1024]{1,0:T(1,128)} %bitcast.19, ...), custom_call_target="tpu_custom_call" | custom-call | tf_op jit(solution)/shard_map/project/pallas_call | solution.py:313
  41.1 134.3 %all_to_all.10 = bf16[32,82,2,128]{3,2,1,0:T(2,128)(2,1)S(1)} all-to-all(bf16[32,82,2,128]{3,2,1,0:T(2,128)(2,1)S(1)} %bitcast.15), channel_id=1, replica_groups=mesh['groups'=4,'dp'=2,'seq'=32] {'seq'}, dimensions={0} | all-to-all | bytes 2686976 | tf_op jit(solution)/shard_map/all_to_all | solution.py:310
  175.4 0.0 copy-start
  175.4 0.0 copy-start.1
  175.4 0.0 copy-start.2
  175.4 0.0 copy-start.3
  175.4 0.0 copy-start.4
  175.5 10.1 %attend.1 = bf16[2176,128]{1,0:T(8,128)(2,1)S(1)} custom-call(bf16[5248,128]{1,0:T(8,128)(2,1)S(1)} %bitcast.10), custom_call_target="tpu_custom_call" | custom-call | tf_op jit(solution)/shard_map/attend/pallas_call | solution.py:341
  185.5 47.8 %all_to_all.11 = bf16[32,34,2,128]{3,2,1,0:T(2,128)(2,1)S(1)} all-to-all(bf16[32,34,2,128]{3,2,1,0:T(2,128)(2,1)S(1)} %bitcast.12), channel_id=1, replica_groups=mesh['groups'=4,'dp'=2,'seq'=32] {'seq'}, dimensions={0} | all-to-all | bytes 1114112 | tf_op jit(solution)/shard_map/all_to_all | solution.py:310
  233.4 0.0 copy-done
  233.4 0.0 copy-done.1
  233.4 0.0 copy-done.2
  233.4 0.0 copy-done.3
  233.4 0.0 copy-done.4
  233.4 2.0 combine.1
Async XLA Ops:
  175.4 58.0 %copy-start = (bf16[1024,1024]{1,0:T(8,128)(2,1)S(1)}, bf16[1024,1024]{1,0:T(8,128)(2,1)}, u32[]{:S(2)}) copy-start(bf16[1024,1024]{1,0:T(8,128)(2,1)} %weight_ref.1) | copy-start | bytes 6291460
  175.4 58.0 %copy-start.1 = (bf16[2,96,1024]{2,1,0:T(8,128)(2,1)S(1)}, bf16[2,96,1024]{2,1,0:T(8,128)(2,1)}, u32[]{:S(2)}) copy-start(bf16[2,96,1024]{2,1,0:T(8,128)(2,1)} %param.8) | copy-start | bytes 1179652
  175.4 58.0 %copy-start.2 = (bf16[1,64,1024]{2,1,0:T(8,128)(2,1)S(1)}, bf16[1,64,1024]{2,1,0:T(8,128)(2,1)}, u32[]{:S(2)}) copy-start(bf16[1,64,1024]{2,1,0:T(8,128)(2,1)} %param.9) | copy-start | bytes 393220
  175.4 58.0 %copy-start.3 = (f32[1024]{0:T(1024)S(1)}, f32[1024]{0:T(1024)}, u32[]{:S(2)}) copy-start(f32[1024]{0:T(1024)} %param.15) | copy-start | bytes 12292
  175.4 58.0 %copy-start.4 = (s32[1,64]{1,0:T(1,128)S(1)}, s32[1,64]{1,0:T(1,128)}, u32[]{:S(2)}) copy-start(s32[1,64]{1,0:T(1,128)} %owner_ref.1) | copy-start | bytes 772

commit v4 on v3

--- a/solution.py
+++ b/solution.py
@@ -68,15 +68,14 @@
     gain_hbm,
     weight_hbm,
     send_ref,
+    normed_ref,
     gate_ref,
-    cgate_ref,
     lengths_ref,
     hist_ref,
     cand_ref,
     owner_ref,
     gain_ref,
     weight_ref,
-    normed_ref,
     loaded,
     arrived,
 ):
@@ -110,30 +109,24 @@
     for load in loads:
         load.start()
     for step in range(steps):
-        for part in (2, 3, 1, 0):
+        for part in (2, 3, 1):
             fetch(step, part).start()
     for load in loads:
         load.wait()
-    @pl.when(lax.axis_index(stagger_axis) > 0)
-    def _():
-        pl.delay(STAGGER_NS)
-
     gain = gain_ref[...]
     normed_ref[:hist_rows] = rms_apply(hist_ref[...].astype(F32), gain).astype(BF16)
     normed_ref[hist_rows:] = rms_apply(cand_ref[...].astype(F32), gain).astype(BF16)
     picks = [selection(owner_ref[...], member) for member in range(hist_local)]
     position = lax.axis_index(axis) * tok_share + lax.broadcasted_iota(jnp.int32, (tok_share, LANES), 0)
 
+    def times(step, rows, part):
+        fetch(step, part).wait()
+        return jnp.dot(normed_ref[:rows], weight_ref[step, part], preferred_element_type=F32)
+
     for step in range(steps):
-
-        def times(rows, part):
-            fetch(step, part).wait()
-            return jnp.dot(normed_ref[:rows], weight_ref[step, part], preferred_element_type=F32)
-
-        all_rows = normed_ref.shape[0]
-        keys = times(hist_rows, 2)
-        values = times(hist_rows, 3)
-        query = times(all_rows, 1).astype(BF16).astype(F32) * (0.5 * HD ** (-0.5))
+        keys = times(step, hist_rows, 2)
+        values = times(step, hist_rows, 3)
+        query = times(step, normed_ref.shape[0], 1).astype(BF16).astype(F32) * (0.5 * HD ** (-0.5))
         cand_query = query[hist_rows:].astype(BF16)
         for member in range(hist_local):
             rows = slice(member * tok_share, (member + 1) * tok_share)
@@ -155,10 +148,15 @@
                 even, odd = even + half, odd + half
                 send_ref[even : even + CAND_HALF] = join(top, swap_halves(low)).astype(BF16)[:CAND_HALF]
                 send_ref[odd : odd + CAND_HALF] = join(swap_halves(top), low).astype(BF16)[:CAND_HALF]
-        gate = silu(times(all_rows, 0)).astype(BF16)
-        columns = slice(step * step_width, (step + 1) * step_width)
-        gate_ref[:, columns] = gate[:hist_rows]
-        cgate_ref[:, columns] = gate[hist_rows:]
+
+    @pl.when(lax.axis_index(stagger_axis) > 0)
+    def _():
+        for step in range(steps):
+            fetch(step, 0).start()
+        for step in range(steps):
+            columns = slice(step * step_width, (step + 1) * step_width)
+            gate_ref[:, columns] = silu(times(step, normed_ref.shape[0], 0)).astype(BF16)
+        pl.delay(STAGGER_NS)
 
 
 def attend_kernel(tok_share, recv_ref, back_ref, kv_ref, vt_ref, q_ref, cq_ref, ot_ref, ct_ref):
@@ -218,8 +216,8 @@
         own = slice(base, base + queries_group)
         part = weigh(group, q_ref[own], causal)
         ot_ref[:, own] = part if group == 0 else ot_ref[:, own] + part
-        if group + 1 < groups:
-            later = slice(base + queries_group, groups * queries_group)
+        for after in range(group + 1, groups):
+            later = slice(after * queries_group, (after + 1) * queries_group)
             part = weigh(group, q_ref[later])
             ot_ref[:, later] = part if group == 0 else ot_ref[:, later] + part
 
@@ -238,19 +236,39 @@
 
 
 def output_kernel(
+    stagger_axis,
     tok_share,
     back_ref,
     owner_ref,
     hist_ref,
     cand_ref,
-    gate_ref,
-    cgate_ref,
+    normed_ref,
+    given_ref,
     gain_ref,
     weight_ref,
+    weight_in_hbm,
     hist_out_ref,
     cand_out_ref,
     rows_ref,
+    gate_ref,
+    gate_weight_ref,
+    arrived,
 ):
+    width = hist_ref.shape[1]
+    is_first = lax.axis_index(stagger_axis) == 0
+
+    @pl.when(is_first)
+    def _():
+        fetch = pltpu.make_async_copy(weight_in_hbm.at[:, :width], gate_weight_ref, arrived)
+        fetch.start()
+        fetch.wait()
+        product = jnp.dot(normed_ref[...], gate_weight_ref[...], preferred_element_type=F32)
+        gate_ref[...] = silu(product).astype(BF16)
+
+    @pl.when(jnp.logical_not(is_first))
+    def _():
+        gate_ref[...] = given_ref[...]
+
     half = tok_share // 2
     hist_rows = hist_ref.shape[0]
     hist_local = hist_rows // tok_share
@@ -280,9 +298,7 @@
     gain = gain_ref[...]
     attended = rows_ref[...]
     scaled = rms_apply(attended, gain)
-    hist_gated = (scaled[:hist_rows] * gate_ref[...].astype(F32)).astype(BF16)
-    cand_gated = (scaled[hist_rows:] * cgate_ref[...].astype(F32)).astype(BF16)
-    gated = jnp.concatenate([hist_gated, cand_gated], axis=0)
+    gated = (scaled * gate_ref[...].astype(F32)).astype(BF16)
     product = jnp.dot(gated, weight_ref[...], preferred_element_type=F32)
     hist_out_ref[...] = (hist_ref[...].astype(F32) + product[:hist_rows]).astype(BF16)
     cand_out_ref[...] = (cand_ref[...].astype(F32) + product[hist_rows:]).astype(BF16)
@@ -310,14 +326,15 @@
         moved = lax.all_to_all(pairs, "seq", split_axis=0, concat_axis=0, tiled=True)
         return pltpu.with_memory_space_constraint(moved.reshape(rows.shape), pltpu.VMEM)
 
-    send, gate, cgate = pl.pallas_call(
+    all_rows = hist_rows + cand_count
+    send, normed, gate = pl.pallas_call(
         functools.partial(project_kernel, "seq", "dp", tok_share),
         in_specs=[pl.BlockSpec(memory_space=pltpu.HBM)] * 6,
         out_specs=[vmem] * 3,
         out_shape=[
             pltpu.VMEM((items * send_rows, LANES), BF16),
-            jax.ShapeDtypeStruct((hist_rows, width), BF16),
-            jax.ShapeDtypeStruct((cand_count, width), BF16),
+            pltpu.VMEM((all_rows, width), BF16),
+            jax.ShapeDtypeStruct((all_rows, width), BF16),
         ],
         scratch_shapes=[
             pltpu.SMEM(lengths.shape, lengths.dtype),
@@ -326,7 +343,6 @@
             pltpu.VMEM(assignment.shape, assignment.dtype),
             pltpu.VMEM(gain_in.shape, F32),
             pltpu.VMEM((H // HEADS_STEP, PARTS, width, HEADS_STEP * HD), BF16),
-            pltpu.VMEM((hist_rows + cand_count, width), BF16),
             pltpu.SemaphoreType.DMA((5,)),
             pltpu.SemaphoreType.DMA((H // HEADS_STEP, PARTS)),
         ],
@@ -355,17 +371,32 @@
         name="attend",
     )(exchange(send))
     hist_out, cand_out = pl.pallas_call(
-        functools.partial(output_kernel, tok_share),
-        in_specs=[vmem] * 8,
+        functools.partial(output_kernel, "dp", tok_share),
+        in_specs=[vmem] * 8 + [pl.BlockSpec(memory_space=pltpu.HBM)],
         out_specs=[vmem] * 2,
         out_shape=[
             jax.ShapeDtypeStruct((hist_rows, width), BF16),
             jax.ShapeDtypeStruct((cand_count, width), BF16),
         ],
-        scratch_shapes=[pltpu.VMEM((hist_rows + cand_count, width), F32)],
+        scratch_shapes=[
+            pltpu.VMEM((all_rows, width), F32),
+            pltpu.VMEM((all_rows, width), BF16),
+            pltpu.VMEM((width, width), BF16),
+            pltpu.SemaphoreType.DMA,
+        ],
         compiler_params=params,
         name="combine",
-    )(exchange(back), assignment, hist, cand, gate, cgate, gain_attn, weight_out)
+    )(
+        exchange(back),
+        assignment,
+        hist,
+        cand,
+        normed,
+        gate,
+        gain_attn,
+        weight_out,
+        pltpu.with_memory_space_constraint(weight_in, pltpu.HBM),
+    )
     return hist_out.reshape(history.shape), cand_out.reshape(candidates.shape)
 
 

time: 236 us -> 234 us (level)
  blocking collectives: 182 us -> 179 us
    all_to_all x2, blocking collectives: 182 us -> 179 us  [exchange(): lax.all_to_all(pairs, 'seq', split_axis=0, concat_axis=0, tiled=True)]
where the time goes in v4:
time: 234 us
  blocking collectives  179 us (76%)
  Pallas kernels  53.5 us (23%)
    all_to_all x2, blocking collectives, exchange(): lax.all_to_all(pairs, 'seq', split_axis=0, concat_axis=0, tiled=True)  179 us
    pallas_call x1, Pallas kernels, per_device(): pl.pallas_call(functools.partial(project_kernel, 'seq', 'dp', tok_share),...  41.8 us
    pallas_call x1, Pallas kernels, per_device(): pl.pallas_call(functools.partial(attend_kernel, tok_share), in_specs=[vme...  9.7 us

profile of v4, /device:TPU:37, one launch (start us, length us, event | category | flops | bytes accessed | tf_op | source)
XLA Modules:
  0.0 233.7 jit_solution(17881264467021434990)
XLA Ops:
  0.6 41.8 %project.1 = (bf16[5248,128]{1,0:T(8,128)(2,1)S(1)}, bf16[256,1024]{1,0:T(8,128)(2,1)S(1)}, bf16[256,1024]{1,0:T(8,128)(2,1)S(1)}) custom-call(s32[2]{0:T(128)} %lengths_hbm.1, bf16[192,1024]{1,0:T(8,128)(2,1)} %bitcast.13, bf16[64,1024]{1,0:T(8,128)(2,1)} %bitcast.16, s32[1,64]{1,0:T(1,128)} %owner_ref.1, f32[1,1024]{1,0:T(1,128)} %bitcast.19, ...), custom_call_target="tpu_custom_call" | custom-call | tf_op jit(solution)/shard_map/project/pallas_call | solution.py:330
  42.4 131.8 %all_to_all.10 = bf16[32,82,2,128]{3,2,1,0:T(2,128)(2,1)S(1)} all-to-all(bf16[32,82,2,128]{3,2,1,0:T(2,128)(2,1)S(1)} %bitcast.15), channel_id=1, replica_groups=mesh['groups'=4,'dp'=2,'seq'=32] {'seq'}, dimensions={0} | all-to-all | bytes 2686976 | tf_op jit(solution)/shard_map/all_to_all | solution.py:326
  174.2 0.0 copy-start
  174.2 0.0 copy-start.1
  174.2 0.0 copy-start.2
  174.2 0.0 copy-start.3
  174.3 0.0 copy-start.4
  174.3 9.7 %attend.1 = bf16[2176,128]{1,0:T(8,128)(2,1)S(1)} custom-call(bf16[5248,128]{1,0:T(8,128)(2,1)S(1)} %bitcast.10), custom_call_target="tpu_custom_call" | custom-call | tf_op jit(solution)/shard_map/attend/pallas_call | solution.py:357
  184.0 47.6 %all_to_all.11 = bf16[32,34,2,128]{3,2,1,0:T(2,128)(2,1)S(1)} all-to-all(bf16[32,34,2,128]{3,2,1,0:T(2,128)(2,1)S(1)} %bitcast.12), channel_id=1, replica_groups=mesh['groups'=4,'dp'=2,'seq'=32] {'seq'}, dimensions={0} | all-to-all | bytes 1114112 | tf_op jit(solution)/shard_map/all_to_all | solution.py:326
  231.5 0.0 copy-done
  231.5 0.0 copy-done.1
  231.5 0.0 copy-done.2
  231.6 0.0 copy-done.3
  231.6 0.0 copy-done.4
  231.6 2.0 combine.1
Async XLA Ops:
  174.2 57.3 %copy-start = (bf16[1024,1024]{1,0:T(8,128)(2,1)S(1)}, bf16[1024,1024]{1,0:T(8,128)(2,1)}, u32[]{:S(2)}) copy-start(bf16[1024,1024]{1,0:T(8,128)(2,1)} %weight_ref.1) | copy-start | bytes 6291460
  174.2 57.3 %copy-start.1 = (bf16[2,96,1024]{2,1,0:T(8,128)(2,1)S(1)}, bf16[2,96,1024]{2,1,0:T(8,128)(2,1)}, u32[]{:S(2)}) copy-start(bf16[2,96,1024]{2,1,0:T(8,128)(2,1)} %param.8) | copy-start | bytes 1179652
  174.2 57.3 %copy-start.2 = (bf16[1,64,1024]{2,1,0:T(8,128)(2,1)S(1)}, bf16[1,64,1024]{2,1,0:T(8,128)(2,1)}, u32[]{:S(2)}) copy-start(bf16[1,64,1024]{2,1,0:T(8,128)(2,1)} %param.9) | copy-start | bytes 393220
  174.2 57.3 %copy-start.3 = (f32[1024]{0:T(1024)S(1)}, f32[1024]{0:T(1024)}, u32[]{:S(2)}) copy-start(f32[1024]{0:T(1024)} %param.15) | copy-start | bytes 12292
  174.3 57.3 %copy-start.4 = (s32[1,64]{1,0:T(1,128)S(1)}, s32[1,64]{1,0:T(1,128)}, u32[]{:S(2)}) copy-start(s32[1,64]{1,0:T(1,128)} %owner_ref.1) | copy-start | bytes 772

commit v5 on v4

--- a/solution.py
+++ b/solution.py
@@ -16,7 +16,8 @@
 HEADS_STEP = 16
 PARTS = 4
 VMEM_LIMIT = 28 << 20
-STAGGER_NS = 35_000
+STAGGER_NS = 32_000
+WEIGHTS_AHEAD = 2
 GROUP = 8
 F32 = jnp.float32
 BF16 = jnp.bfloat16
@@ -190,19 +191,6 @@
     for group in range(groups):
         vt_ref[group] = keys_of(group).T[HD:]
 
-    def weigh(group, query, allowed=None):
-        half_score = lax.dot_general(
-            keys_of(group), query, (((1,), (1,)), ((), ())), preferred_element_type=F32
-        )
-        weight = half_score + half_score * jnp.tanh(half_score)
-        if allowed is not None:
-            weight = jnp.where(allowed, weight, 0.0)
-        return jnp.dot(vt_ref[group], weight.astype(BF16), preferred_element_type=F32)
-
-    for group in range(groups):
-        part = weigh(group, cq_ref[...])
-        ct_ref[...] = part if group == 0 else ct_ref[...] + part
-
     column = lax.broadcasted_iota(jnp.int32, (1, queries_group), 1)
     is_low = (column >= half_group).astype(jnp.int32)
     column = column - is_low * half_group
@@ -211,15 +199,32 @@
         source = source + (column >= later * half).astype(jnp.int32)
     position = source * half + column + is_low * half
     causal = lax.broadcasted_iota(jnp.int32, (keys_group, queries_group), 0) <= position
+
+    def weights(group, query, allowed):
+        half_score = lax.dot_general(
+            keys_of(group), query, (((1,), (1,)), ((), ())), preferred_element_type=F32
+        )
+        weight = half_score + half_score * jnp.tanh(half_score)
+        if allowed is not None:
+            weight = jnp.where(allowed, weight, 0.0)
+        return weight.astype(BF16)
+
+    def gather(ref, columns, group, weight, first):
+        part = jnp.dot(vt_ref[group], weight, preferred_element_type=F32)
+        ref[:, columns] = part if first else ref[:, columns] + part
+
+    work = [(ct_ref, slice(0, 2 * cands), group, cq_ref, None, group == 0) for group in range(groups)]
     for group in range(groups):
-        base = group * queries_group
-        own = slice(base, base + queries_group)
-        part = weigh(group, q_ref[own], causal)
-        ot_ref[:, own] = part if group == 0 else ot_ref[:, own] + part
-        for after in range(group + 1, groups):
-            later = slice(after * queries_group, (after + 1) * queries_group)
-            part = weigh(group, q_ref[later])
-            ot_ref[:, later] = part if group == 0 else ot_ref[:, later] + part
+        for after in range(group, groups):
+            columns = slice(after * queries_group, (after + 1) * queries_group)
+            work.append((ot_ref, columns, group, q_ref, causal if after == group else None, group == 0))
+    pending = []
+    for ref, columns, group, query_ref, allowed, first in work:
+        pending.append((ref, columns, group, weights(group, query_ref[columns], allowed), first))
+        if len(pending) > WEIGHTS_AHEAD:
+            gather(*pending.pop(0))
+    for waiting in pending:
+        gather(*waiting)
 
     for group in range(groups):
         base = group * queries_group

time: 234 us -> 233 us (level)
  Pallas kernels: 53.5 us -> 50.2 us
  blocking collectives: 179 us -> 182 us
    pallas_call x1, Pallas kernels: 41.8 us -> 38.8 us  [per_device(): pl.pallas_call(functools.partial(project_kernel, 'seq', 'dp', tok_share),...]
    all_to_all x2, blocking collectives: 179 us -> 182 us  [exchange(): lax.all_to_all(pairs, 'seq', split_axis=0, concat_axis=0, tiled=True)]
where the time goes in v5:
time: 233 us
  blocking collectives  182 us (78%)
  Pallas kernels  50.2 us (22%)
    all_to_all x2, blocking collectives, exchange(): lax.all_to_all(pairs, 'seq', split_axis=0, concat_axis=0, tiled=True)  182 us
    pallas_call x1, Pallas kernels, per_device(): pl.pallas_call(functools.partial(project_kernel, 'seq', 'dp', tok_share),...  38.8 us
    pallas_call x1, Pallas kernels, per_device(): pl.pallas_call(functools.partial(attend_kernel, tok_share), in_specs=[vme...  9.41 us

profile of v5, /device:TPU:37, one launch (start us, length us, event | category | flops | bytes accessed | tf_op | source)
XLA Modules:
  0.0 233.3 jit_solution(4972847254018604882)
XLA Ops:
  0.6 38.8 %project.1 = (bf16[5248,128]{1,0:T(8,128)(2,1)S(1)}, bf16[256,1024]{1,0:T(8,128)(2,1)S(1)}, bf16[256,1024]{1,0:T(8,128)(2,1)S(1)}) custom-call(s32[2]{0:T(128)} %lengths_hbm.1, bf16[192,1024]{1,0:T(8,128)(2,1)} %bitcast.13, bf16[64,1024]{1,0:T(8,128)(2,1)} %bitcast.16, s32[1,64]{1,0:T(1,128)} %owner_ref.1, f32[1,1024]{1,0:T(1,128)} %bitcast.19, ...), custom_call_target="tpu_custom_call" | custom-call | tf_op jit(solution)/shard_map/project/pallas_call | solution.py:335
  39.4 134.9 %all_to_all.10 = bf16[32,82,2,128]{3,2,1,0:T(2,128)(2,1)S(1)} all-to-all(bf16[32,82,2,128]{3,2,1,0:T(2,128)(2,1)S(1)} %bitcast.15), channel_id=1, replica_groups=mesh['groups'=4,'dp'=2,'seq'=32] {'seq'}, dimensions={0} | all-to-all | bytes 2686976 | tf_op jit(solution)/shard_map/all_to_all | solution.py:331
  174.4 0.0 copy-start
  174.4 0.0 copy-start.1
  174.4 0.0 copy-start.2
  174.4 0.0 copy-start.3
  174.4 0.0 copy-start.4
  174.4 9.4 %attend.1 = bf16[2176,128]{1,0:T(8,128)(2,1)S(1)} custom-call(bf16[5248,128]{1,0:T(8,128)(2,1)S(1)} %bitcast.10), custom_call_target="tpu_custom_call" | custom-call | tf_op jit(solution)/shard_map/attend/pallas_call | solution.py:362
  183.8 47.2 %all_to_all.11 = bf16[32,34,2,128]{3,2,1,0:T(2,128)(2,1)S(1)} all-to-all(bf16[32,34,2,128]{3,2,1,0:T(2,128)(2,1)S(1)} %bitcast.12), channel_id=1, replica_groups=mesh['groups'=4,'dp'=2,'seq'=32] {'seq'}, dimensions={0} | all-to-all | bytes 1114112 | tf_op jit(solution)/shard_map/all_to_all | solution.py:331
  231.0 0.0 copy-done
  231.1 0.0 copy-done.1
  231.1 0.0 copy-done.2
  231.1 0.0 copy-done.3
  231.1 0.0 copy-done.4
  231.1 2.0 combine.1
Async XLA Ops:
  174.4 56.7 %copy-start = (bf16[1024,1024]{1,0:T(8,128)(2,1)S(1)}, bf16[1024,1024]{1,0:T(8,128)(2,1)}, u32[]{:S(2)}) copy-start(bf16[1024,1024]{1,0:T(8,128)(2,1)} %weight_ref.1) | copy-start | bytes 6291460
  174.4 56.7 %copy-start.1 = (bf16[2,96,1024]{2,1,0:T(8,128)(2,1)S(1)}, bf16[2,96,1024]{2,1,0:T(8,128)(2,1)}, u32[]{:S(2)}) copy-start(bf16[2,96,1024]{2,1,0:T(8,128)(2,1)} %param.8) | copy-start | bytes 1179652
  174.4 56.7 %copy-start.2 = (bf16[1,64,1024]{2,1,0:T(8,128)(2,1)S(1)}, bf16[1,64,1024]{2,1,0:T(8,128)(2,1)}, u32[]{:S(2)}) copy-start(bf16[1,64,1024]{2,1,0:T(8,128)(2,1)} %param.9) | copy-start | bytes 393220
  174.4 56.7 %copy-start.3 = (f32[1024]{0:T(1024)S(1)}, f32[1024]{0:T(1024)}, u32[]{:S(2)}) copy-start(f32[1024]{0:T(1024)} %param.15) | copy-start | bytes 12292
  174.4 56.7 %copy-start.4 = (s32[1,64]{1,0:T(1,128)S(1)}, s32[1,64]{1,0:T(1,128)}, u32[]{:S(2)}) copy-start(s32[1,64]{1,0:T(1,128)} %owner_ref.1) | copy-start | bytes 772

commit v6 on v5

--- a/solution.py
+++ b/solution.py
@@ -71,6 +71,7 @@
     send_ref,
     normed_ref,
     gate_ref,
+    picks_ref,
     lengths_ref,
     hist_ref,
     cand_ref,
@@ -118,6 +119,8 @@
     normed_ref[:hist_rows] = rms_apply(hist_ref[...].astype(F32), gain).astype(BF16)
     normed_ref[hist_rows:] = rms_apply(cand_ref[...].astype(F32), gain).astype(BF16)
     picks = [selection(owner_ref[...], member) for member in range(hist_local)]
+    for member in range(hist_local):
+        picks_ref[member] = picks[member]
     position = lax.axis_index(axis) * tok_share + lax.broadcasted_iota(jnp.int32, (tok_share, LANES), 0)
 
     def times(step, rows, part):
@@ -244,7 +247,7 @@
     stagger_axis,
     tok_share,
     back_ref,
-    owner_ref,
+    picks_ref,
     hist_ref,
     cand_ref,
     normed_ref,
@@ -279,7 +282,6 @@
     hist_local = hist_rows // tok_share
     cand_rows = cand_ref.shape[0]
     chunk = half + CAND_HALF
-    picks = [selection(owner_ref[...], member) for member in range(hist_local)]
     fill = jnp.zeros((CAND_PAD - CAND_HALF, LANES), F32)
     for pair in range(H // 2):
         lanes = slice(pair * LANES, (pair + 1) * LANES)
@@ -297,7 +299,7 @@
             upper, lower = join(even, swap_halves(odd)), join(swap_halves(even), odd)
             found = jnp.concatenate([upper, fill, lower, fill], axis=0).astype(BF16)
             cross_slab = cross_slab + lax.dot_general(
-                picks[member], found, (((0,), (0,)), ((), ())), preferred_element_type=F32
+                picks_ref[member], found, (((0,), (0,)), ((), ())), preferred_element_type=F32
             )
         rows_ref[hist_rows:, lanes] = cross_slab
     gain = gain_ref[...]
@@ -332,14 +334,15 @@
         return pltpu.with_memory_space_constraint(moved.reshape(rows.shape), pltpu.VMEM)
 
     all_rows = hist_rows + cand_count
-    send, normed, gate = pl.pallas_call(
+    send, normed, gate, picks = pl.pallas_call(
         functools.partial(project_kernel, "seq", "dp", tok_share),
         in_specs=[pl.BlockSpec(memory_space=pltpu.HBM)] * 6,
-        out_specs=[vmem] * 3,
+        out_specs=[vmem] * 4,
         out_shape=[
             pltpu.VMEM((items * send_rows, LANES), BF16),
             pltpu.VMEM((all_rows, width), BF16),
             jax.ShapeDtypeStruct((all_rows, width), BF16),
+            pltpu.VMEM((hist_local, 2 * CAND_PAD, cand_count), BF16),
         ],
         scratch_shapes=[
             pltpu.SMEM(lengths.shape, lengths.dtype),
@@ -393,7 +396,7 @@
         name="combine",
     )(
         exchange(back),
-        assignment,
+        picks,
         hist,
         cand,
         normed,

time: 233 us -> 233 us (level)
  no operation moved by 1% of the time
where the time goes in v6:
time: 233 us
  blocking collectives  182 us (78%)
  Pallas kernels  50.2 us (22%)
    all_to_all x2, blocking collectives, exchange(): lax.all_to_all(pairs, 'seq', split_axis=0, concat_axis=0, tiled=True)  182 us
    pallas_call x1, Pallas kernels, per_device(): pl.pallas_call(functools.partial(project_kernel, 'seq', 'dp', tok_share),...  38.8 us
    pallas_call x1, Pallas kernels, per_device(): pl.pallas_call(functools.partial(attend_kernel, tok_share), in_specs=[vme...  9.41 us

profile of v6, /device:TPU:37, one launch (start us, length us, event | category | flops | bytes accessed | tf_op | source)
XLA Modules:
  0.0 233.2 jit_solution(15830137943014552220)
XLA Ops:
  0.6 38.8 %project.1 = (bf16[5248,128]{1,0:T(8,128)(2,1)S(1)}, bf16[256,1024]{1,0:T(8,128)(2,1)S(1)}, bf16[256,1024]{1,0:T(8,128)(2,1)S(1)}, bf16[2,48,64]{2,1,0:T(8,128)(2,1)S(1)}) custom-call(s32[2]{0:T(128)} %lengths_hbm.1, bf16[192,1024]{1,0:T(8,128)(2,1)} %bitcast.13, bf16[64,1024]{1,0:T(8,128)(2,1)} %bitcast.16, s32[1,64]{1,0:T(1,128)} %owner_hbm.1, ...), custom_call_target="tpu_custom_call" | custom-call | tf_op jit(solution)/shard_map/project/pallas_call | solution.py:337
  39.4 134.9 %all_to_all.10 = bf16[32,82,2,128]{3,2,1,0:T(2,128)(2,1)S(1)} all-to-all(bf16[32,82,2,128]{3,2,1,0:T(2,128)(2,1)S(1)} %bitcast.15), channel_id=1, replica_groups=mesh['groups'=4,'dp'=2,'seq'=32] {'seq'}, dimensions={0} | all-to-all | bytes 2686976 | tf_op jit(solution)/shard_map/all_to_all | solution.py:333
  174.3 0.0 copy-start
  174.4 0.0 copy-start.1
  174.4 0.0 copy-start.2
  174.4 0.0 copy-start.3
  174.4 9.4 %attend.1 = bf16[2176,128]{1,0:T(8,128)(2,1)S(1)} custom-call(bf16[5248,128]{1,0:T(8,128)(2,1)S(1)} %bitcast.10), custom_call_target="tpu_custom_call" | custom-call | tf_op jit(solution)/shard_map/attend/pallas_call | solution.py:365
  183.8 47.3 %all_to_all.11 = bf16[32,34,2,128]{3,2,1,0:T(2,128)(2,1)S(1)} all-to-all(bf16[32,34,2,128]{3,2,1,0:T(2,128)(2,1)S(1)} %bitcast.12), channel_id=1, replica_groups=mesh['groups'=4,'dp'=2,'seq'=32] {'seq'}, dimensions={0} | all-to-all | bytes 1114112 | tf_op jit(solution)/shard_map/all_to_all | solution.py:333
  231.1 0.0 copy-done
  231.1 0.0 copy-done.1
  231.1 0.0 copy-done.2
  231.1 0.0 copy-done.3
  231.1 2.0 combine.1
Async XLA Ops:
  174.3 56.7 %copy-start = (bf16[1024,1024]{1,0:T(8,128)(2,1)S(1)}, bf16[1024,1024]{1,0:T(8,128)(2,1)}, u32[]{:S(2)}) copy-start(bf16[1024,1024]{1,0:T(8,128)(2,1)} %weight_ref.1) | copy-start | bytes 6291460
  174.4 56.7 %copy-start.1 = (bf16[2,96,1024]{2,1,0:T(8,128)(2,1)S(1)}, bf16[2,96,1024]{2,1,0:T(8,128)(2,1)}, u32[]{:S(2)}) copy-start(bf16[2,96,1024]{2,1,0:T(8,128)(2,1)} %param.8) | copy-start | bytes 1179652
  174.4 56.7 %copy-start.2 = (bf16[1,64,1024]{2,1,0:T(8,128)(2,1)S(1)}, bf16[1,64,1024]{2,1,0:T(8,128)(2,1)}, u32[]{:S(2)}) copy-start(bf16[1,64,1024]{2,1,0:T(8,128)(2,1)} %param.9) | copy-start | bytes 393220
  174.4 56.7 %copy-start.3 = (f32[1024]{0:T(1024)S(1)}, f32[1024]{0:T(1024)}, u32[]{:S(2)}) copy-start(f32[1024]{0:T(1024)} %param.15) | copy-start | bytes 12292
